TPU v7x, 512 devices: a whole 4x4x16 slice. The times are simulated.
512 devices in a mesh: gx: 32 (over y, x, core), gy: 16 (over z).
Axes of the slice: x: 4, y: 4, z: 16, core: 2. Of those that a mesh axis runs over, the one named last changes fastest.
Arguments:
- snapshots: bfloat16 [131072, 2048], P(('gx', 'gy')), may hold values from -6 to 6
- volume: bfloat16 [65536, 2048], P('gx', 'gy'), may hold values from -6 to 6
- start_basis: bfloat16 [64, 131072], P(None, ('gx', 'gy')), may hold values from -6 to 6
- wake_mask: int32 [2048], P(('gx', 'gy')), may hold values 0 or 1
Outputs:
- plane_modes: float32 [64, 131072], P(None, ('gx', 'gy'))
- wake_modes: float32 [64, 65536], P(None, ('gx', 'gy'))
All inputs are finite; a program needn't handle non-finite values. No bound on the sum of `wake_mask` on one device may be relied on, other than what follows from the above.
Results may differ from a plain program's by a relative error of at most 0.018.
Values may be sent and summed in bfloat16 or wider, within the bound.
No kernel may reach another device: no remote copies, remote signals or barrier semaphores. Data moves between devices by JAX's collectives and lax.ppermute only.
A program may use at most 64 MiB of HBM per device.

v0:
```python
import jax
import jax.numpy as jnp
from jax import lax
from jax.sharding import Mesh
from jax.sharding import PartitionSpec as P

ITERS = 3
CBLOCK = 32
GX_GY = ("gx_0", "gx_1", "gx_2", "gy")
GX = ("gx_0", "gx_1", "gx_2")


def one_axis_at_a_time(array, axes):
    for axis in axes:
        array = lax.psum(array, axis)
    return array


def cut_along(array, dim, count):
    lengths = array.shape
    tiles = array.reshape(*lengths[:dim], count, lengths[dim] // count, *lengths[dim + 1 :])
    return jnp.moveaxis(tiles, dim, 0)


def sent_and_summed(array, axis, dim):
    tiles = cut_along(array, dim, lax.axis_size(axis))
    arrived = lax.all_to_all(tiles, axis, split_axis=0, concat_axis=0, tiled=True)
    return arrived.sum(axis=0)


def summed_rows(array, axes, dim):
    far, near = axes
    tiles = cut_along(array, dim, lax.axis_size(far))
    nearer = sent_and_summed(tiles, near, dim + 1)
    arrived = lax.all_to_all(nearer, far, split_axis=0, concat_axis=0, tiled=True)
    return arrived.sum(axis=0)


def filled_up(lines, count):
    spare = -len(lines) % count
    return jnp.pad(lines, [(0, spare)] + [(0, 0)] * (lines.ndim - 1))


def copy_for_each(array, axis):
    copies = jnp.broadcast_to(array, (lax.axis_size(axis), *array.shape))
    return lax.all_to_all(copies, axis, split_axis=0, concat_axis=0, tiled=True)


def laid_out(tiles, dim):
    tiles = jnp.moveaxis(tiles, 0, dim)
    lengths = tiles.shape
    return tiles.reshape(*lengths[:dim], lengths[dim] * lengths[dim + 1], *lengths[dim + 2 :])


def gather_axes(array, axes, dim):
    far, near = axes
    tiles = copy_for_each(copy_for_each(array, far), near)
    return laid_out(tiles.swapaxes(0, 1).reshape(-1, *array.shape), dim)


def sum_by_parts(array, axes):
    lines = array.reshape(-1)
    own = summed_rows(filled_up(lines, lax.axis_size(axes[0]) * lax.axis_size(axes[1])), axes, 0)
    whole = gather_axes(own, axes, 0)
    return whole[: len(lines)].reshape(array.shape)


def triangular(lower, right):
    return jax.scipy.linalg.solve_triangular(lower, right, lower=True)


def temporal_weights(basis, snapshots):
    gram_part = jnp.dot(basis, basis.T, preferred_element_type=jnp.float32)
    coeff_part = jnp.dot(basis, snapshots, preferred_element_type=jnp.float32)
    gram = one_axis_at_a_time(gram_part, GX_GY)
    lower = jnp.linalg.cholesky(gram)
    weights = sum_by_parts(triangular(lower, coeff_part), (("gx_0", "gx_1"), ("gx_2", "gy")))
    return (lower, weights)


def local(snapshots, volume, start_basis, wake_mask):
    basis = start_basis
    for step in range(ITERS):
        lower, weights = temporal_weights(basis, snapshots)
        weights_b = weights.astype(jnp.bfloat16)
        basis = lax.dot_general(
            weights_b, snapshots, (((1,), (1,)), ((), ())), preferred_element_type=jnp.float32
        ).astype(jnp.bfloat16)
    lower, weights = temporal_weights(basis, snapshots)
    total_points = snapshots.shape[0] * lax.axis_size(GX) * lax.axis_size("gy")
    plane_modes = triangular(lower, basis.astype(jnp.float32)) * jnp.sqrt(jnp.float32(total_points))
    norms = jnp.sqrt(jnp.sum(weights * weights, axis=1, keepdims=True))
    scaled = (weights / norms).astype(jnp.bfloat16)
    own_cells = lax.all_to_all(volume, "gy", split_axis=0, concat_axis=1, tiled=True)
    projection = lax.dot_general(
        scaled, own_cells, (((1,), (1,)), ((), ())), preferred_element_type=jnp.float32
    )
    cell_mask = jnp.repeat(wake_mask, CBLOCK).astype(jnp.float32)
    return (plane_modes, projection * cell_mask[None, :])


def solution(mesh):
    finer = Mesh(mesh.devices.reshape(4, 4, 2, mesh.shape["gy"]), ("gx_0", "gx_1", "gx_2", "gy"))
    placed = (P(GX_GY, None), P(GX, "gy"), P(None, GX_GY), P(GX_GY))
    return jax.shard_map(
        local,
        mesh=finer,
        in_specs=placed,
        out_specs=(P(None, GX_GY), P(None, GX_GY)),
        check_vma=False,
    )
```

profile of v0, /device:TPU:1, one launch (start us, length us, event | category | flops | bytes accessed | tf_op | source)
XLA Modules:
  0.0 810.1 jit_solution(11774204600463809200)
XLA Ops:
  0.6 1.0 fusion.25
  1.6 14.4 %psum.112 = f32[64,64]{0,1:T(8,128)S(1)} all-reduce(f32[64,64]{0,1:T(8,128)S(1)} %fusion.25), channel_id=1, replica_groups=mesh['gx_0'=4,'gx_1'=4,'gx_2'=2,'gy'=16] {'gx_0'}, use_global_device_ids=true, to_apply=%region_0.0 | all-reduce | flops 4096 | bytes 32768 | tf_op jit(solution)/shard_map/psum | solution.py:15
  16.1 13.3 %psum.113 = f32[64,64]{0,1:T(8,128)S(1)} all-reduce(f32[64,64]{0,1:T(8,128)S(1)} %psum.112), channel_id=1, replica_groups=mesh['gx_0'=4,'gx_1'=4,'gx_2'=2,'gy'=16] {'gx_1'}, use_global_device_ids=true, to_apply=%region_1.0 | all-reduce | flops 4096 | bytes 32768 | tf_op jit(solution)/shard_map/psum | solution.py:15
  29.3 11.4 %psum.114 = f32[64,64]{0,1:T(8,128)S(1)} all-reduce(f32[64,64]{0,1:T(8,128)S(1)} %psum.113), channel_id=1, replica_groups=mesh['gx_0'=4,'gx_1'=4,'gx_2'=2,'gy'=16] {'gx_2'}, use_global_device_ids=true, to_apply=%region_2.0 | all-reduce | flops 4096 | bytes 32768 | tf_op jit(solution)/shard_map/psum | solution.py:15
  40.8 48.2 %psum.115 = f32[64,64]{0,1:T(8,128)S(1)} all-reduce(f32[64,64]{0,1:T(8,128)S(1)} %psum.114), channel_id=1, replica_groups=mesh['gx_0'=4,'gx_1'=4,'gx_2'=2,'gy'=16] {'gy'}, use_global_device_ids=true, to_apply=%region_3.0 | all-reduce | flops 4096 | bytes 32768 | tf_op jit(solution)/shard_map/psum | solution.py:15
  89.0 5.8 cholesky.74
  94.9 0.6 compare_reduce_fusion.3
  95.6 0.7 fusion.2
  96.2 4.9 custom-call.13
  101.5 0.6 fusion.16
  102.5 51.0 %all_to_all.131 = f32[32,16,256]{2,1,0:T(8,128)S(1)} all-to-all(f32[32,16,256]{2,1,0:T(8,128)S(1)} %bitcast.116), channel_id=1, replica_groups=mesh['gx_0'=4,'gx_1'=4,'gx_2'=2,'gy'=16] {'gx_2','gy'}, dimensions={0} | all-to-all | bytes 1048576 | tf_op jit(solution)/shard_map/all_to_all | solution.py:27
  153.5 9.7 %all_to_all.132 = f32[16,1,256]{2,1,0:T(1,128)S(1)} all-to-all(f32[16,1,256]{2,1,0:T(1,128)S(1)} %all_to_all.87), channel_id=1, replica_groups=mesh['gx_0'=4,'gx_1'=4,'gx_2'=2,'gy'=16] {'gx_0','gx_1'}, dimensions={0} | all-to-all | bytes 32768 | tf_op jit(solution)/shard_map/all_to_all | solution.py:35
  163.2 0.5 broadcast.69
  163.7 0.7 reduce.10
  164.4 9.5 %all_to_all.133 = bf16[16,2,128]{2,1,0:T(2,128)(2,1)S(1)} all-to-all(bf16[16,2,128]{2,1,0:T(2,128)(2,1)S(1)} %reshape.72), channel_id=1, replica_groups=mesh['gx_0'=4,'gx_1'=4,'gx_2'=2,'gy'=16] {'gx_0','gx_1'}, dimensions={0} | all-to-all | bytes 16384 | tf_op jit(solution)/shard_map/all_to_all | solution.py:46
  174.0 30.0 %all_to_all.134 = bf16[32,16,256]{2,1,0:T(8,128)(2,1)S(1)} all-to-all(bf16[32,16,256]{2,1,0:T(8,128)(2,1)S(1)} %broadcast_in_dim.31), channel_id=1, replica_groups=mesh['gx_0'=4,'gx_1'=4,'gx_2'=2,'gy'=16] {'gx_2','gy'}, dimensions={0} | all-to-all | bytes 524288 | tf_op jit(solution)/shard_map/all_to_all | solution.py:46
  205.0 11.7 %psum.116 = f32[64,64]{0,1:T(8,128)S(1)} all-reduce(f32[64,64]{0,1:T(8,128)S(1)} %fusion.27), channel_id=1, replica_groups=mesh['gx_0'=4,'gx_1'=4,'gx_2'=2,'gy'=16] {'gx_0'}, use_global_device_ids=true, to_apply=%region_8.11 | all-reduce | flops 4096 | bytes 32768 | tf_op jit(solution)/shard_map/psum | solution.py:15
  216.8 11.7 %psum.117 = f32[64,64]{0,1:T(8,128)S(1)} all-reduce(f32[64,64]{0,1:T(8,128)S(1)} %psum.116), channel_id=1, replica_groups=mesh['gx_0'=4,'gx_1'=4,'gx_2'=2,'gy'=16] {'gx_1'}, use_global_device_ids=true, to_apply=%region_9.12 | all-reduce | flops 4096 | bytes 32768 | tf_op jit(solution)/shard_map/psum | solution.py:15
  228.5 9.7 %psum.118 = f32[64,64]{0,1:T(8,128)S(1)} all-reduce(f32[64,64]{0,1:T(8,128)S(1)} %psum.117), channel_id=1, replica_groups=mesh['gx_0'=4,'gx_1'=4,'gx_2'=2,'gy'=16] {'gx_2'}, use_global_device_ids=true, to_apply=%region_10.13 | all-reduce | flops 4096 | bytes 32768 | tf_op jit(solution)/shard_map/psum | solution.py:15
  238.2 40.2 %psum.119 = f32[64,64]{0,1:T(8,128)S(1)} all-reduce(f32[64,64]{0,1:T(8,128)S(1)} %psum.118), channel_id=1, replica_groups=mesh['gx_0'=4,'gx_1'=4,'gx_2'=2,'gy'=16] {'gy'}, use_global_device_ids=true, to_apply=%region_11.14 | all-reduce | flops 4096 | bytes 32768 | tf_op jit(solution)/shard_map/psum | solution.py:15
  278.5 5.8 cholesky.85
  284.4 0.6 compare_reduce_fusion.2
  285.0 0.7 fusion.3
  285.7 4.9 custom-call.14
  290.6 0.6 fusion.13
  291.6 49.8 %all_to_all.135 = f32[32,16,256]{2,1,0:T(8,128)S(1)} all-to-all(f32[32,16,256]{2,1,0:T(8,128)S(1)} %bitcast.117), channel_id=1, replica_groups=mesh['gx_0'=4,'gx_1'=4,'gx_2'=2,'gy'=16] {'gx_2','gy'}, dimensions={0} | all-to-all | bytes 1048576 | tf_op jit(solution)/shard_map/all_to_all | solution.py:27
  341.5 9.7 %all_to_all.136 = f32[16,1,256]{2,1,0:T(1,128)S(1)} all-to-all(f32[16,1,256]{2,1,0:T(1,128)S(1)} %all_to_all.93), channel_id=1, replica_groups=mesh['gx_0'=4,'gx_1'=4,'gx_2'=2,'gy'=16] {'gx_0','gx_1'}, dimensions={0} | all-to-all | bytes 32768 | tf_op jit(solution)/shard_map/all_to_all | solution.py:35
  351.2 0.7 reduce.11
  351.9 9.5 %all_to_all.137 = bf16[16,2,128]{2,1,0:T(2,128)(2,1)S(1)} all-to-all(bf16[16,2,128]{2,1,0:T(2,128)(2,1)S(1)} %reshape.74), channel_id=1, replica_groups=mesh['gx_0'=4,'gx_1'=4,'gx_2'=2,'gy'=16] {'gx_0','gx_1'}, dimensions={0} | all-to-all | bytes 16384 | tf_op jit(solution)/shard_map/all_to_all | solution.py:46
  361.4 29.9 %all_to_all.138 = bf16[32,16,256]{2,1,0:T(8,128)(2,1)S(1)} all-to-all(bf16[32,16,256]{2,1,0:T(8,128)(2,1)S(1)} %broadcast_in_dim.33), channel_id=1, replica_groups=mesh['gx_0'=4,'gx_1'=4,'gx_2'=2,'gy'=16] {'gx_2','gy'}, dimensions={0} | all-to-all | bytes 524288 | tf_op jit(solution)/shard_map/all_to_all | solution.py:46
  391.5 0.4 convolution_convert_fusion.1
  392.4 11.7 %psum.120 = f32[64,64]{0,1:T(8,128)S(1)} all-reduce(f32[64,64]{0,1:T(8,128)S(1)} %fusion.29), channel_id=1, replica_groups=mesh['gx_0'=4,'gx_1'=4,'gx_2'=2,'gy'=16] {'gx_0'}, use_global_device_ids=true, to_apply=%region_14.17 | all-reduce | flops 4096 | bytes 32768 | tf_op jit(solution)/shard_map/psum | solution.py:15
  404.1 12.1 %psum.121 = f32[64,64]{0,1:T(8,128)S(1)} all-reduce(f32[64,64]{0,1:T(8,128)S(1)} %psum.120), channel_id=1, replica_groups=mesh['gx_0'=4,'gx_1'=4,'gx_2'=2,'gy'=16] {'gx_1'}, use_global_device_ids=true, to_apply=%region_15.18 | all-reduce | flops 4096 | bytes 32768 | tf_op jit(solution)/shard_map/psum | solution.py:15
  416.2 10.1 %psum.122 = f32[64,64]{0,1:T(8,128)S(1)} all-reduce(f32[64,64]{0,1:T(8,128)S(1)} %psum.121), channel_id=1, replica_groups=mesh['gx_0'=4,'gx_1'=4,'gx_2'=2,'gy'=16] {'gx_2'}, use_global_device_ids=true, to_apply=%region_16.19 | all-reduce | flops 4096 | bytes 32768 | tf_op jit(solution)/shard_map/psum | solution.py:15
  426.3 39.8 %psum.123 = f32[64,64]{0,1:T(8,128)S(1)} all-reduce(f32[64,64]{0,1:T(8,128)S(1)} %psum.122), channel_id=1, replica_groups=mesh['gx_0'=4,'gx_1'=4,'gx_2'=2,'gy'=16] {'gy'}, use_global_device_ids=true, to_apply=%region_17.20 | all-reduce | flops 4096 | bytes 32768 | tf_op jit(solution)/shard_map/psum | solution.py:15
  466.2 5.8 cholesky.96
  472.1 0.6 compare_reduce_fusion.1
  472.7 0.7 fusion.4
  473.4 4.9 custom-call.15
  478.3 0.6 fusion.10
  479.3 49.5 %all_to_all.139 = f32[32,16,256]{2,1,0:T(8,128)S(1)} all-to-all(f32[32,16,256]{2,1,0:T(8,128)S(1)} %bitcast.118), channel_id=1, replica_groups=mesh['gx_0'=4,'gx_1'=4,'gx_2'=2,'gy'=16] {'gx_2','gy'}, dimensions={0} | all-to-all | bytes 1048576 | tf_op jit(solution)/shard_map/all_to_all | solution.py:27
  528.9 9.7 %all_to_all.140 = f32[16,1,256]{2,1,0:T(1,128)S(1)} all-to-all(f32[16,1,256]{2,1,0:T(1,128)S(1)} %all_to_all.99), channel_id=1, replica_groups=mesh['gx_0'=4,'gx_1'=4,'gx_2'=2,'gy'=16] {'gx_0','gx_1'}, dimensions={0} | all-to-all | bytes 32768 | tf_op jit(solution)/shard_map/all_to_all | solution.py:35
  538.6 0.7 reduce.12
  539.3 9.5 %all_to_all.141 = bf16[16,2,128]{2,1,0:T(2,128)(2,1)S(1)} all-to-all(bf16[16,2,128]{2,1,0:T(2,128)(2,1)S(1)} %reshape.76), channel_id=1, replica_groups=mesh['gx_0'=4,'gx_1'=4,'gx_2'=2,'gy'=16] {'gx_0','gx_1'}, dimensions={0} | all-to-all | bytes 16384 | tf_op jit(solution)/shard_map/all_to_all | solution.py:46
  548.8 30.0 %all_to_all.142 = bf16[32,16,256]{2,1,0:T(8,128)(2,1)S(1)} all-to-all(bf16[32,16,256]{2,1,0:T(8,128)(2,1)S(1)} %broadcast_in_dim.35), channel_id=1, replica_groups=mesh['gx_0'=4,'gx_1'=4,'gx_2'=2,'gy'=16] {'gx_2','gy'}, dimensions={0} | all-to-all | bytes 524288 | tf_op jit(solution)/shard_map/all_to_all | solution.py:46
  579.9 11.7 %psum.124 = f32[64,64]{0,1:T(8,128)S(1)} all-reduce(f32[64,64]{0,1:T(8,128)S(1)} %fusion.31), channel_id=1, replica_groups=mesh['gx_0'=4,'gx_1'=4,'gx_2'=2,'gy'=16] {'gx_0'}, use_global_device_ids=true, to_apply=%region_20.23 | all-reduce | flops 4096 | bytes 32768 | tf_op jit(solution)/shard_map/psum | solution.py:15
  591.6 11.7 %psum.125 = f32[64,64]{0,1:T(8,128)S(1)} all-reduce(f32[64,64]{0,1:T(8,128)S(1)} %psum.124), channel_id=1, replica_groups=mesh['gx_0'=4,'gx_1'=4,'gx_2'=2,'gy'=16] {'gx_1'}, use_global_device_ids=true, to_apply=%region_21.24 | all-reduce | flops 4096 | bytes 32768 | tf_op jit(solution)/shard_map/psum | solution.py:15
  603.4 9.7 %psum.126 = f32[64,64]{0,1:T(8,128)S(1)} all-reduce(f32[64,64]{0,1:T(8,128)S(1)} %psum.125), channel_id=1, replica_groups=mesh['gx_0'=4,'gx_1'=4,'gx_2'=2,'gy'=16] {'gx_2'}, use_global_device_ids=true, to_apply=%region_22.25 | all-reduce | flops 4096 | bytes 32768 | tf_op jit(solution)/shard_map/psum | solution.py:15
  613.1 40.2 %psum.127 = f32[64,64]{0,1:T(8,128)S(1)} all-reduce(f32[64,64]{0,1:T(8,128)S(1)} %psum.126), channel_id=1, replica_groups=mesh['gx_0'=4,'gx_1'=4,'gx_2'=2,'gy'=16] {'gy'}, use_global_device_ids=true, to_apply=%region_23.26 | all-reduce | flops 4096 | bytes 32768 | tf_op jit(solution)/shard_map/psum | solution.py:15
  653.4 5.8 cholesky.107
  659.2 0.6 compare_reduce_fusion
  659.9 0.7 fusion.5
  660.5 4.9 custom-call.9
  665.4 0.6 fusion.6
  666.5 49.8 %all_to_all.143 = f32[32,16,256]{2,1,0:T(8,128)S(1)} all-to-all(f32[32,16,256]{2,1,0:T(8,128)S(1)} %bitcast.119), channel_id=1, replica_groups=mesh['gx_0'=4,'gx_1'=4,'gx_2'=2,'gy'=16] {'gx_2','gy'}, dimensions={0} | all-to-all | bytes 1048576 | tf_op jit(solution)/shard_map/all_to_all | solution.py:27
  716.3 9.7 %all_to_all.144 = f32[16,1,256]{2,1,0:T(1,128)S(1)} all-to-all(f32[16,1,256]{2,1,0:T(1,128)S(1)} %all_to_all.105), channel_id=1, replica_groups=mesh['gx_0'=4,'gx_1'=4,'gx_2'=2,'gy'=16] {'gx_0','gx_1'}, dimensions={0} | all-to-all | bytes 32768 | tf_op jit(solution)/shard_map/all_to_all | solution.py:35
  726.0 9.5 %all_to_all.145 = f32[16,1,256]{2,1,0:T(1,128)S(1)} all-to-all(f32[16,1,256]{2,1,0:T(1,128)S(1)} %broadcast_in_dim.36), channel_id=1, replica_groups=mesh['gx_0'=4,'gx_1'=4,'gx_2'=2,'gy'=16] {'gx_0','gx_1'}, dimensions={0} | all-to-all | bytes 32768 | tf_op jit(solution)/shard_map/all_to_all | solution.py:46
  735.5 5.1 all-to-all-start.16
  740.6 22.5 %all-to-all-done.16 = bf16[16,128,128]{2,1,0:T(8,128)(2,1)S(1)} async-done(((bf16[16,128,128]{2,1,0:T(8,128)(2,1)}), bf16[16,128,128]{2,1,0:T(8,128)(2,1)S(1)}, u32[]{:S(2)}, u32[]{:S(2)}) %all-to-all-start.16) | async-done | bytes 524320 | tf_op jit(solution)/shard_map/all_to_all | solution.py:94
  763.1 0.8 broadcast_in_dim.37
  764.0 14.1 %all-to-all-start.15 = ((f32[32,16,256]{2,1,0:T(8,128)}), f32[32,16,256]{2,1,0:T(8,128)S(1)}, u32[]{:S(2)}, u32[]{:S(2)}) async-start(f32[32,16,256]{2,1,0:T(8,128)} %broadcast_in_dim.37), calls=%async_computation.15 | async-start | bytes 1048576 | tf_op jit(solution)/shard_map/all_to_all | solution.py:46
  778.5 0.9 convolution_multiply_fusion
  779.4 29.0 %all-to-all-done.15 = f32[32,16,256]{2,1,0:T(8,128)S(1)} async-done(((f32[32,16,256]{2,1,0:T(8,128)}), f32[32,16,256]{2,1,0:T(8,128)S(1)}, u32[]{:S(2)}, u32[]{:S(2)}) %all-to-all-start.15) | async-done | bytes 524320 | tf_op jit(solution)/shard_map/all_to_all | solution.py:46
  809.3 0.8 convolution_multiply_fusion.1
  (85 shorter events, 7.1 us)
Async XLA Ops:
  0.6 100.5 %copy-start = (bf16[256,2048]{1,0:T(8,128)(2,1)S(1)}, bf16[256,2048]{1,0:T(8,128)(2,1)}, u32[]{:S(2)}) copy-start(bf16[256,2048]{1,0:T(8,128)(2,1)} %param.7) | copy-start | bytes 3145732
  95.6 5.6 copy-start.1
  735.5 27.6 %all-to-all-start.16 = ((bf16[16,128,128]{2,1,0:T(8,128)(2,1)}), bf16[16,128,128]{2,1,0:T(8,128)(2,1)S(1)}, u32[]{:S(2)}, u32[]{:S(2)}) async-start(bf16[16,128,128]{2,1,0:T(8,128)(2,1)} %bitcast.23), calls=%async_computation.16 | async-start | bytes 1048576 | tf_op jit(solution)/shard_map/all_to_all | solution.py:94
  764.0 14.1 %copy-start.2 = (s32[4]{0:T(128)S(1)}, s32[4]{0:T(128)}, u32[]{:S(2)}) copy-start(s32[4]{0:T(128)} %param.10) | copy-start | bytes 52
  764.0 44.4 %all-to-all-start.15 = ((f32[32,16,256]{2,1,0:T(8,128)}), f32[32,16,256]{2,1,0:T(8,128)S(1)}, u32[]{:S(2)}, u32[]{:S(2)}) async-start(f32[32,16,256]{2,1,0:T(8,128)} %broadcast_in_dim.37), calls=%async_computation.15 | async-start | bytes 1048576 | tf_op jit(solution)/shard_map/all_to_all | solution.py:46
where the time goes:
time: 812 us; the launch traced here: 810 us
  blocking collectives  674 us (83%)
  waiting for transfers between devices  51.4 us (6%)
  other arithmetic  51.1 us (6%)
  starting transfers between devices  19.2 us (2%)
  matrix products  8.17 us (1%)
    psum x16, blocking collectives, one_axis_at_a_time(): array = lax.psum(array, axis)  308 us
    all_to_all x4, blocking collectives, sent_and_summed(): lax.all_to_all(tiles, axis, split_axis=0, concat_axis=0, tiled=True)  200 us
    all_to_all x7, blocking collectives, copy_for_each(): return lax.all_to_all(copies, axis, split_axis=0, concat_axis=0, tiled=True)  128 us
    all_to_all x4, blocking collectives, summed_rows(): lax.all_to_all(nearer, far, split_axis=0, concat_axis=0, tiled=True)  38.6 us
    all_to_all x1, waiting for transfers between devices, copy_for_each(): return lax.all_to_all(copies, axis, split_axis=0, concat_axis=0, tiled=True)  29 us
    another operation x12, other arithmetic, temporal_weights(): lower = jnp.linalg.cholesky(gram)  26.1 us
    all_to_all x1, waiting for transfers between devices, local(): lax.all_to_all(volume, 'gy', split_axis=0, concat_axis=1, tiled=True)  22.5 us
    another operation x8, other arithmetic, triangular(): return jax.scipy.linalg.solve_triangular(lower, right, lower=True)  22.2 us
  transfers between devices with their start and end apart: 2, of which 2 were waited for; matrix products, arithmetic and copies ran while one was open for 0% of the time, Pallas kernels for 0%

commit v1 on v0

v1 whole, which is shorter than its diff:
```python
import functools

import jax
import jax.numpy as jnp
from jax import lax
from jax.experimental import pallas as pl
from jax.experimental.pallas import tpu as pltpu
from jax.sharding import Mesh
from jax.sharding import PartitionSpec as P

ITERS = 3
CBLOCK = 32
PLANE = ("gx_0", "gx_1", "gx_2")
EVERY = ("gx_0", "gx_1", "gx_2", "gy")
PANEL = 4
f32 = jnp.float32
bf16 = jnp.bfloat16
ROW_BY_ROW = (((1,), (1,)), ((), ()))


def whitener(gram):
    n = gram.shape[0]
    blocks = n // 8
    lane = lax.broadcasted_iota(jnp.int32, (8, 2 * n), 1)
    sub = lax.broadcasted_iota(jnp.int32, (8, 2 * n), 0)
    wide = jnp.concatenate([gram, jnp.zeros((n, n), f32)], axis=1)
    rows = [jnp.where(lane == sub + (n + 8 * b), 1.0, wide[8 * b : 8 * b + 8]) for b in range(blocks)]
    scale = [jnp.zeros((8, 2 * n), f32) for _ in range(blocks)]
    for start in range(0, n, PANEL):
        b = start // 8
        cols = [
            [jnp.broadcast_to(rows[r][:, k : k + 1], (8, 2 * n)) for r in range(b, blocks)]
            for k in range(start, start + PANEL)
        ]
        for j in range(PANEL):
            s = (start + j) % 8
            pivot = jnp.broadcast_to(cols[j][0][s : s + 1], (8, 2 * n))
            inverse = 1.0 / pivot
            scale[b] = jnp.where(sub == s, lax.rsqrt(pivot), scale[b])
            line = jnp.broadcast_to(rows[b][s : s + 1], (8, 2 * n)) * inverse
            below = jnp.where(sub > s, cols[j][0], 0.0)
            for i in range(j + 1, PANEL):
                t = (start + i) % 8
                factor = jnp.broadcast_to(cols[j][0][t : t + 1], (8, 2 * n)) * inverse
                cols[i][0] = cols[i][0] - below * factor
                for r in range(1, blocks - b):
                    cols[i][r] = cols[i][r] - cols[j][r] * factor
            rows[b] = rows[b] - below * line
            for r in range(1, blocks - b):
                rows[b + r] = rows[b + r] - cols[j][r] * line
    full = jnp.concatenate([r * s for r, s in zip(rows, scale)], axis=0)
    return full[:, n:]


def high_and_low(value):
    high = value.astype(bf16)
    return high, (value - high.astype(f32)).astype(bf16)


def whiten(gathered, previous, stack, white):
    modes = stack.shape[0] // 3
    half = modes // 2
    for q in range(stack.shape[1] // 128):
        span = slice(128 * q, 128 * q + 128)
        for side in range(2):
            high, low = high_and_low(gathered[2 * q + side, :half, :])
            stack[half * side : half * side + half, span] = high
            stack[modes + half * side : modes + half * side + half, span] = high
            stack[2 * modes + half * side : 2 * modes + half * side + half, span] = low
    if previous is None:
        lines = jnp.concatenate([gathered[p, half : half + 1, :] for p in range(half)], axis=0)
        gram = jnp.concatenate([lines[:, :modes], lines[:, modes:]], axis=0)
    else:
        both = lax.dot_general(stack[modes:, :], previous[...], ROW_BY_ROW, preferred_element_type=f32)
        gram = both[:modes] + both[modes:]
    inverse = whitener(gram)
    high, low = high_and_low(inverse)
    white[...] = jnp.concatenate([high, low, high], axis=1)
    weights = jnp.dot(white[...], stack[...], preferred_element_type=f32)
    return weights, high, low


def project(basis, rows, parts):
    coeff = jnp.dot(basis, rows[...], preferred_element_type=f32).astype(bf16)
    half = coeff.shape[0] // 2
    for q in range(coeff.shape[1] // 128):
        for side in range(2):
            parts[2 * q + side, :half, :] = coeff[half * side : half * side + half, 128 * q : 128 * q + 128]


def first_step(start, rows, parts):
    basis = start[...]
    modes = basis.shape[0]
    half = modes // 2
    gram = lax.dot_general(basis, basis, ROW_BY_ROW, preferred_element_type=f32)
    lines = jnp.concatenate([gram[:half], gram[half:]], axis=1)
    high, low = high_and_low(lines)
    least = (lines - high.astype(f32) - low.astype(f32)).astype(bf16)
    spare = jnp.zeros((parts.shape[1] - half - 3, 128), bf16)
    for p in range(half):
        own = slice(p, p + 1)
        parts[p, half:, :] = jnp.concatenate([high[own], low[own], least[own], spare], axis=0)
    project(basis, rows, parts)


def next_step(with_gram, *refs):
    if with_gram:
        gathered, rows, parts, weights_b, new_basis, stack, white = refs
        previous = None
    else:
        gathered, previous, rows, parts, weights_b, new_basis, stack, white = refs
    weights, _, _ = whiten(gathered, previous, stack, white)
    weights_b[...] = weights.astype(bf16)
    basis = lax.dot_general(weights_b[...], rows[...], ROW_BY_ROW, preferred_element_type=f32).astype(bf16)
    new_basis[...] = basis
    project(basis, rows, parts)


def last_step(root, gathered, previous, basis, cells, mask, plane, wake, stack, white):
    weights, high, low = whiten(gathered, previous, stack, white)
    modes = high.shape[0]
    twice = jnp.concatenate([high, low], axis=0)
    both = jnp.dot(twice, basis[...], preferred_element_type=f32)
    plane[...] = (both[:modes] + both[modes:]) * root
    norms = jnp.sqrt(jnp.sum(weights * weights, axis=1, keepdims=True))
    scaled = (weights / norms).astype(bf16)
    projection = lax.dot_general(scaled, cells[...], ROW_BY_ROW, preferred_element_type=f32)
    wake[...] = projection * mask[...]


def call(body, outs, scratch, *args):
    return pl.pallas_call(
        body,
        out_shape=outs,
        scratch_shapes=scratch,
        name=body.func.__name__ if isinstance(body, functools.partial) else body.__name__,
    )(*args)


def copies_to_each(array, axes):
    copies = jnp.broadcast_to(array, (lax.axis_size(axes), *array.shape))
    return lax.all_to_all(copies, axes, split_axis=0, concat_axis=0, tiled=True)


def summed(parts, with_gram):
    arrived = lax.all_to_all(parts, PLANE, split_axis=0, concat_axis=0, tiled=True)
    own = arrived.astype(f32).sum(axis=0)
    if with_gram:
        half = 32
        gram = own[half : half + 1] + own[half + 1 : half + 2] + own[half + 2 : half + 3]
        own = jnp.concatenate([own[:half], gram, jnp.zeros((7, 128), f32)], axis=0)
    own = copies_to_each(own, "gy").sum(axis=0)
    return copies_to_each(own, PLANE)


def local(snapshots, volume, start_basis, wake_mask):
    points, snaps = snapshots.shape
    modes = start_basis.shape[0]
    half = modes // 2
    pieces = 2 * snaps // 128
    plain = jax.ShapeDtypeStruct((pieces, half, 128), bf16)
    scratch = [pltpu.VMEM((3 * modes, snaps), bf16), pltpu.VMEM((modes, 3 * modes), bf16)]
    parts = call(first_step, jax.ShapeDtypeStruct((pieces, half + 16, 128), bf16), [], start_basis, snapshots)
    gathered = summed(parts, True)
    weights_b = None
    for step in range(ITERS):
        outs = (plain, jax.ShapeDtypeStruct((modes, snaps), bf16), jax.ShapeDtypeStruct((modes, points), bf16))
        given = (gathered,) if weights_b is None else (gathered, weights_b)
        parts, weights_b, basis = call(
            functools.partial(next_step, weights_b is None), outs, scratch, *given, snapshots
        )
        gathered = summed(parts, False)
    own_cells = lax.all_to_all(volume, "gy", split_axis=0, concat_axis=1, tiled=True)
    cell_mask = jnp.repeat(wake_mask, CBLOCK).astype(f32)[None, :]
    total_points = points * lax.axis_size(EVERY)
    outs = (jax.ShapeDtypeStruct((modes, points), f32), jax.ShapeDtypeStruct((modes, own_cells.shape[0]), f32))
    return call(
        functools.partial(last_step, float(total_points) ** 0.5),
        outs, scratch, gathered, weights_b, basis, own_cells, cell_mask,
    )


def solution(mesh):
    finer = Mesh(mesh.devices.reshape(4, 4, 2, mesh.shape["gy"]), EVERY)
    placed = (P(EVERY, None), P(PLANE, "gy"), P(None, EVERY), P(EVERY))
    return jax.shard_map(
        local,
        mesh=finer,
        in_specs=placed,
        out_specs=(P(None, EVERY), P(None, EVERY)),
        check_vma=False,
    )
```

time: 812 us -> 295 us (0.36)
  blocking collectives: 674 us -> 188 us
  other arithmetic: 51.1 us -> 0.39 us
  Pallas kernels: 0 us -> 26.9 us
  starting transfers between devices: 19.2 us -> 31.2 us
  waiting for transfers between devices: 51.4 us -> 43 us
  matrix products: 8.17 us -> 0 us
    psum x16 -> x0, blocking collectives: 308 us -> none  [one_axis_at_a_time(): array = lax.psum(array, axis)]
    all_to_all x15 -> x10, blocking collectives: 366 us -> 188 us  [the longest x7 150 us: copies_to_each(): return lax.all_to_all(copies, axes, split_axis=0, concat_axis=0, tiled=True)]
    another operation x20 -> x0, other arithmetic: 48.3 us -> none  [the longest x12 26.1 us: temporal_weights(): lower = jnp.linalg.cholesky(gram)]
    pallas_call x0 -> x5, Pallas kernels: none -> 26.9 us  [call(): pl.pallas_call(body, out_shape=outs, scratch_shapes=scratch, name=body.fu...]
    all_to_all x1 -> x2, waiting for transfers between devices: 29 us -> 20.1 us  [the longest x1 10.2 us: summed(): lax.all_to_all(parts, PLANE, split_axis=0, concat_axis=0, tiled=True)]
    all_to_all x1 -> x2, starting transfers between devices: 14.1 us -> 21.1 us  [the longest x1 10.7 us: copies_to_each(): return lax.all_to_all(copies, axes, split_axis=0, concat_axis=0, tiled=True)]
  transfers between devices with their start and end apart: 2 -> 3, of which waited for: 2 -> 3; matrix products, arithmetic and copies ran while one was open for 0% -> 1% of each run, Pallas kernels for 0% -> 0%
where the time goes in v1:
time: 295 us; the launch traced here: 294 us
  blocking collectives  188 us (64%)
  waiting for transfers between devices  43 us (15%)
  starting transfers between devices  31.2 us (11%)
  Pallas kernels  26.9 us (9%)
  local copies, waits for them, and re-layouts  3.59 us (1%)
    all_to_all x7, blocking collectives, copies_to_each(): return lax.all_to_all(copies, axes, split_axis=0, concat_axis=0, tiled=True)  150 us
    all_to_all x3, blocking collectives, summed(): lax.all_to_all(parts, PLANE, split_axis=0, concat_axis=0, tiled=True)  38.8 us
    pallas_call x5, Pallas kernels, call(): pl.pallas_call(body, out_shape=outs, scratch_shapes=scratch, name=body.fu...  26.9 us
    all_to_all x1, waiting for transfers between devices, local(): lax.all_to_all(volume, 'gy', split_axis=0, concat_axis=1, tiled=True)  22.9 us
    all_to_all x1, starting transfers between devices, copies_to_each(): return lax.all_to_all(copies, axes, split_axis=0, concat_axis=0, tiled=True)  10.7 us
    all_to_all x1, starting transfers between devices, summed(): lax.all_to_all(parts, PLANE, split_axis=0, concat_axis=0, tiled=True)  10.4 us
    all_to_all x1, waiting for transfers between devices, summed(): lax.all_to_all(parts, PLANE, split_axis=0, concat_axis=0, tiled=True)  10.2 us
    all_to_all x1, starting transfers between devices, local(): lax.all_to_all(volume, 'gy', split_axis=0, concat_axis=1, tiled=True)  10.1 us
  transfers between devices with their start and end apart: 3, of which 3 were waited for; matrix products, arithmetic and copies ran while one was open for 1% of the time, Pallas kernels for 0%

profile of v1, /device:TPU:1, one launch (start us, length us, event | category | flops | bytes accessed | tf_op | source)
XLA Modules:
  0.0 294.3 jit_solution(15404548911221733757)
XLA Ops:
  0.6 2.3 first_step.1
  2.9 10.4 %all-to-all-start = ((bf16[32,48,128]{2,1,0:T(8,128)(2,1)}), bf16[32,48,128]{2,1,0:T(8,128)(2,1)S(1)}, u32[]{:S(2)}, u32[]{:S(2)}) async-start(bf16[32,48,128]{2,1,0:T(8,128)(2,1)} %first_step.1), calls=%async_computation | async-start | bytes 786432 | tf_op jit(solution)/shard_map/all_to_all | solution.py:146
  13.3 0.1 pad.2.clone
  13.4 10.2 %all-to-all-done = bf16[32,48,128]{2,1,0:T(8,128)(2,1)S(1)} async-done(((bf16[32,48,128]{2,1,0:T(8,128)(2,1)}), bf16[32,48,128]{2,1,0:T(8,128)(2,1)S(1)}, u32[]{:S(2)}, u32[]{:S(2)}) %all-to-all-start) | async-done | bytes 393248 | tf_op jit(solution)/shard_map/all_to_all | solution.py:146
  23.5 0.1 convert_reduce_fusion
  23.6 0.1 maximum_maximum_fusion
  23.7 28.3 %all_to_all.79 = f32[16,40,128]{2,1,0:T(8,128)S(1)} all-to-all(f32[16,40,128]{2,1,0:T(8,128)S(1)} %broadcast_in_dim.32), channel_id=1, replica_groups=mesh['gx_0'=4,'gx_1'=4,'gx_2'=2,'gy'=16] {'gy'}, dimensions={0} | all-to-all | bytes 655360 | tf_op jit(solution)/shard_map/all_to_all | solution.py:142
  52.1 22.8 %all_to_all.80.refs_0_ = f32[32,40,128]{2,1,0:T(8,128)} all-to-all(f32[32,40,128]{2,1,0:T(8,128)S(1)} %broadcast_in_dim.33), channel_id=1, replica_groups=mesh['gx_0'=4,'gx_1'=4,'gx_2'=2,'gy'=16] {'gx_0','gx_1','gx_2'}, dimensions={0} | all-to-all | bytes 1310720 | tf_op jit(solution)/shard_map/all_to_all | solution.py:142
  75.0 6.0 %next_step.3 = (bf16[32,32,128]{2,1,0:T(8,128)(2,1)}, bf16[64,2048]{1,0:T(8,128)(2,1)}, bf16[64,256]{1,0:T(8,128)(2,1)}) custom-call(f32[32,40,128]{2,1,0:T(8,128)} %all_to_all.80.refs_0_, bf16[256,2048]{1,0:T(8,128)(2,1)} %refs_2_.3), custom_call_target="tpu_custom_call" | custom-call | tf_op jit(solution)/shard_map/next_step/pallas_call | solution.py:132
  80.9 13.0 %all_to_all.81 = bf16[32,32,128]{2,1,0:T(8,128)(2,1)S(1)} all-to-all(bf16[32,32,128]{2,1,0:T(8,128)(2,1)} %get-tuple-element.9), channel_id=1, replica_groups=mesh['gx_0'=4,'gx_1'=4,'gx_2'=2,'gy'=16] {'gx_0','gx_1','gx_2'}, dimensions={0} | all-to-all | bytes 524288 | tf_op jit(solution)/shard_map/all_to_all | solution.py:146
  94.0 19.6 %all_to_all.82 = f32[16,32,128]{2,1,0:T(8,128)S(1)} all-to-all(f32[16,32,128]{2,1,0:T(8,128)S(1)} %broadcast_in_dim.34), channel_id=1, replica_groups=mesh['gx_0'=4,'gx_1'=4,'gx_2'=2,'gy'=16] {'gy'}, dimensions={0} | all-to-all | bytes 524288 | tf_op jit(solution)/shard_map/all_to_all | solution.py:142
  113.6 0.1 broadcast_in_dim.35
  113.6 19.8 %all_to_all.83.refs_0_ = f32[32,32,128]{2,1,0:T(8,128)} all-to-all(f32[32,32,128]{2,1,0:T(8,128)S(1)} %broadcast_in_dim.35), channel_id=1, replica_groups=mesh['gx_0'=4,'gx_1'=4,'gx_2'=2,'gy'=16] {'gx_0','gx_1','gx_2'}, dimensions={0} | all-to-all | bytes 1048576 | tf_op jit(solution)/shard_map/all_to_all | solution.py:142
  133.5 6.5 %next_step.4 = (bf16[32,32,128]{2,1,0:T(8,128)(2,1)}, bf16[64,2048]{1,0:T(8,128)(2,1)}, bf16[64,256]{1,0:T(8,128)(2,1)}) custom-call(f32[32,32,128]{2,1,0:T(8,128)} %all_to_all.83.refs_0_, bf16[64,2048]{1,0:T(8,128)(2,1)} %get-tuple-element.10.refs_1_, bf16[256,2048]{1,0:T(8,128)(2,1)} %refs_2_.3), custom_call_target="tpu_custom_call" | custom-call | tf_op jit(solution)/shard_map/next_step/pallas_call | solution.py:132
  140.0 12.9 %all_to_all.84 = bf16[32,32,128]{2,1,0:T(8,128)(2,1)S(1)} all-to-all(bf16[32,32,128]{2,1,0:T(8,128)(2,1)} %get-tuple-element.11), channel_id=1, replica_groups=mesh['gx_0'=4,'gx_1'=4,'gx_2'=2,'gy'=16] {'gx_0','gx_1','gx_2'}, dimensions={0} | all-to-all | bytes 524288 | tf_op jit(solution)/shard_map/all_to_all | solution.py:146
  152.9 19.7 %all_to_all.85 = f32[16,32,128]{2,1,0:T(8,128)S(1)} all-to-all(f32[16,32,128]{2,1,0:T(8,128)S(1)} %broadcast_in_dim.36), channel_id=1, replica_groups=mesh['gx_0'=4,'gx_1'=4,'gx_2'=2,'gy'=16] {'gy'}, dimensions={0} | all-to-all | bytes 524288 | tf_op jit(solution)/shard_map/all_to_all | solution.py:142
  172.6 0.1 broadcast_in_dim.37
  172.7 19.8 %all_to_all.86.refs_0_ = f32[32,32,128]{2,1,0:T(8,128)} all-to-all(f32[32,32,128]{2,1,0:T(8,128)S(1)} %broadcast_in_dim.37), channel_id=1, replica_groups=mesh['gx_0'=4,'gx_1'=4,'gx_2'=2,'gy'=16] {'gx_0','gx_1','gx_2'}, dimensions={0} | all-to-all | bytes 1048576 | tf_op jit(solution)/shard_map/all_to_all | solution.py:142
  192.5 6.5 %next_step.5 = (bf16[32,32,128]{2,1,0:T(8,128)(2,1)}, bf16[64,2048]{1,0:T(8,128)(2,1)}, bf16[64,256]{1,0:T(8,128)(2,1)}) custom-call(f32[32,32,128]{2,1,0:T(8,128)} %all_to_all.86.refs_0_, bf16[64,2048]{1,0:T(8,128)(2,1)} %get-tuple-element.12.refs_1_, bf16[256,2048]{1,0:T(8,128)(2,1)} %refs_2_.3), custom_call_target="tpu_custom_call" | custom-call | tf_op jit(solution)/shard_map/next_step/pallas_call | solution.py:132
  199.0 12.9 %all_to_all.87 = bf16[32,32,128]{2,1,0:T(8,128)(2,1)S(1)} all-to-all(bf16[32,32,128]{2,1,0:T(8,128)(2,1)} %get-tuple-element.13), channel_id=1, replica_groups=mesh['gx_0'=4,'gx_1'=4,'gx_2'=2,'gy'=16] {'gx_0','gx_1','gx_2'}, dimensions={0} | all-to-all | bytes 524288 | tf_op jit(solution)/shard_map/all_to_all | solution.py:146
  212.0 19.7 %all_to_all.88 = f32[16,32,128]{2,1,0:T(8,128)S(1)} all-to-all(f32[16,32,128]{2,1,0:T(8,128)S(1)} %broadcast_in_dim.38), channel_id=1, replica_groups=mesh['gx_0'=4,'gx_1'=4,'gx_2'=2,'gy'=16] {'gy'}, dimensions={0} | all-to-all | bytes 524288 | tf_op jit(solution)/shard_map/all_to_all | solution.py:142
  231.6 10.1 %all-to-all-start.12 = ((bf16[16,128,128]{2,1,0:T(8,128)(2,1)}), bf16[16,128,128]{2,1,0:T(8,128)(2,1)S(1)}, u32[]{:S(2)}, u32[]{:S(2)}) async-start(bf16[16,128,128]{2,1,0:T(8,128)(2,1)} %bitcast), calls=%async_computation.12 | async-start | bytes 1048576 | tf_op jit(solution)/shard_map/all_to_all | solution.py:173
  241.7 22.9 %all-to-all-done.12 = bf16[16,128,128]{2,1,0:T(8,128)(2,1)S(1)} async-done(((bf16[16,128,128]{2,1,0:T(8,128)(2,1)}), bf16[16,128,128]{2,1,0:T(8,128)(2,1)S(1)}, u32[]{:S(2)}, u32[]{:S(2)}) %all-to-all-start.12) | async-done | bytes 524320 | tf_op jit(solution)/shard_map/all_to_all | solution.py:173
  264.7 0.9 broadcast_in_dim.39
  265.5 0.0 copy-start.1
  265.5 10.7 %all-to-all-start.11 = ((f32[32,32,128]{2,1,0:T(8,128)}), f32[32,32,128]{2,1,0:T(8,128)S(1)}, u32[]{:S(2)}, u32[]{:S(2)}) async-start(f32[32,32,128]{2,1,0:T(8,128)} %broadcast_in_dim.39), calls=%async_computation.11 | async-start | bytes 1048576 | tf_op jit(solution)/shard_map/all_to_all | solution.py:142
  276.2 0.0 copy-done.1
  276.3 0.1 broadcast_in_dim.40
  276.3 0.7 convert_element_type.31.mask
  277.0 0.9 copy_bitcast_fusion.cells
  277.9 9.9 %all-to-all-done.11.gathered = f32[32,32,128]{2,1,0:T(8,128)S(1)} async-done(((f32[32,32,128]{2,1,0:T(8,128)}), f32[32,32,128]{2,1,0:T(8,128)S(1)}, u32[]{:S(2)}, u32[]{:S(2)}) %all-to-all-start.11) | async-done | bytes 524320 | tf_op jit(solution)/shard_map/all_to_all | solution.py:142
  287.8 0.0 copy-start
  287.8 0.8 copy-done
  288.6 5.7 %last_step.1 = (f32[64,256]{1,0:T(8,128)}, f32[64,128]{1,0:T(8,128)}) custom-call(f32[32,32,128]{2,1,0:T(8,128)} %copy-done, bf16[64,2048]{1,0:T(8,128)(2,1)} %get-tuple-element.14.previous, bf16[64,256]{1,0:T(8,128)(2,1)} %get-tuple-element.15.basis, bf16[128,2048]{1,0:T(8,128)(2,1)} %copy_bitcast_fusion.cells, f32[1,128]{1,0:T(1,128)} %convert_element_type.31.mask), custom_call_target="tpu_custom_call" | custom-call | tf_op jit(solution)/shard_map/last_step/pallas_call | solution.py:132
  (16 shorter events, 0.4 us)
Async XLA Ops:
  2.9 20.6 %all-to-all-start = ((bf16[32,48,128]{2,1,0:T(8,128)(2,1)}), bf16[32,48,128]{2,1,0:T(8,128)(2,1)S(1)}, u32[]{:S(2)}, u32[]{:S(2)}) async-start(bf16[32,48,128]{2,1,0:T(8,128)(2,1)} %first_step.1), calls=%async_computation | async-start | bytes 786432 | tf_op jit(solution)/shard_map/all_to_all | solution.py:146
  231.6 33.0 %all-to-all-start.12 = ((bf16[16,128,128]{2,1,0:T(8,128)(2,1)}), bf16[16,128,128]{2,1,0:T(8,128)(2,1)S(1)}, u32[]{:S(2)}, u32[]{:S(2)}) async-start(bf16[16,128,128]{2,1,0:T(8,128)(2,1)} %bitcast), calls=%async_computation.12 | async-start | bytes 1048576 | tf_op jit(solution)/shard_map/all_to_all | solution.py:173
  265.5 10.7 %copy-start.1 = (s32[4]{0:T(128)S(1)}, s32[4]{0:T(128)}, u32[]{:S(2)}) copy-start(s32[4]{0:T(128)} %param.7) | copy-start | bytes 52
  265.5 22.3 %all-to-all-start.11 = ((f32[32,32,128]{2,1,0:T(8,128)}), f32[32,32,128]{2,1,0:T(8,128)S(1)}, u32[]{:S(2)}, u32[]{:S(2)}) async-start(f32[32,32,128]{2,1,0:T(8,128)} %broadcast_in_dim.39), calls=%async_computation.11 | async-start | bytes 1048576 | tf_op jit(solution)/shard_map/all_to_all | solution.py:142
  287.8 0.8 copy-start
